TPU v7x, 128 devices: a whole 4x4x4 slice. The times are simulated.
128 devices in a mesh: dp: 1, ep: 128 (over z, y, x, core).
Axes of the slice: x: 4, y: 4, z: 4, core: 2. Of those that a mesh axis runs over, the one named last changes fastest.
Arguments:
- x_in: bfloat16 [32768, 2048], P(('dp', 'ep'))
- expert_ids: int32 [32768, 8], P(('dp', 'ep'))
- norm_weight: bfloat16 [2048], replicated
- router_w: bfloat16 [2048, 128], replicated
- router_b: bfloat16 [128], replicated
- w_gate_up: bfloat16 [128, 2048, 1536], P('ep')
- b_gate_up: bfloat16 [128, 1536], P('ep')
- w_down: bfloat16 [128, 768, 2048], P('ep')
- b_down: bfloat16 [128, 2048], P('ep')
Outputs:
- output: bfloat16 [32768, 2048], P(('dp', 'ep'))
All inputs are finite; a program needn't handle non-finite values.
Results may differ from a plain program's by a relative error of at most 0.00638535.
Values are sent between devices in bfloat16 or wider.
A program may use at most 1 GiB of HBM per device.

v0:
```python
import functools

import jax
import jax.numpy as jnp
from jax import lax
from jax.experimental import pallas as pl
from jax.experimental.pallas import tpu as pltpu
from jax.sharding import Mesh, PartitionSpec as P


CAPACITY_FACTOR = 4
EPSILON = 1e-5
LIMIT = 7.0
ALPHA = 1.702
BLOCK = 256
HALF = BLOCK // 2
GROUP = 2
GATE_JOBS = {
    'za': ((0, 0), (0, 1), (1, 0), (1, 1)),
    'zb': ((2, 0), (4, 1), (3, 0), (5, 1)),
    'zc': ((2, 1), (4, 0), (3, 1), (5, 0)),
    'zd': ((6, 0), (6, 1), (7, 0), (7, 1)),
}
DOWN_JOBS = {'ya': (0, 1), 'yb': (2, 4), 'yc': (3, 5)}
RING = ('z', 'y')
ALL = ('z', 'y', 'x', 'c')


def rms_norm(x_in, norm_weight):
    x_float = x_in.astype(jnp.float32)
    inv_rms = lax.rsqrt(jnp.mean(x_float * x_float, axis=-1, keepdims=True) + EPSILON)
    return (x_float * inv_rms * norm_weight.astype(jnp.float32)).astype(jnp.bfloat16)


def route_gates(hidden, expert_ids, router_w, router_b):
    logits = jnp.dot(hidden, router_w, preferred_element_type=jnp.float32) + router_b.astype(jnp.float32)
    chosen = expert_ids[:, :, None] == jnp.arange(logits.shape[1], dtype=jnp.int32)
    return jax.nn.softmax(jnp.sum(jnp.where(chosen, logits[:, None, :], 0.0), axis=-1), axis=-1)


def even_odd(dtype):
    row = lax.broadcasted_iota(jnp.int32, (BLOCK, BLOCK), 0)
    col = lax.broadcasted_iota(jnp.int32, (BLOCK, BLOCK), 1)
    return (row == jnp.where(col < HALF, 2 * col, 2 * (col - HALF) + 1)).astype(jnp.float32).astype(dtype)


def split_kernel(w_ref, low_ref, high_ref):
    perm = even_odd(jnp.bfloat16)
    per_half = low_ref.shape[1] // BLOCK
    for i in range(2 * per_half):
        out = low_ref if i < per_half else high_ref
        part = jnp.dot(w_ref[0, :, i * BLOCK:(i + 1) * BLOCK], perm, preferred_element_type=jnp.float32)
        j = i % per_half
        out[:, j * BLOCK:(j + 1) * BLOCK] = part.astype(jnp.bfloat16)


def split_columns(w):
    _, rows, cols = w.shape
    tile = rows // 4
    return pl.pallas_call(
        split_kernel,
        grid=(4,),
        in_specs=[pl.BlockSpec((1, tile, cols), lambda i: (0, i, 0))],
        out_specs=[pl.BlockSpec((tile, cols // 2), lambda i: (i, 0))] * 2,
        out_shape=[jax.ShapeDtypeStruct((rows, cols // 2), w.dtype)] * 2,
        cost_estimate=pl.CostEstimate(flops=2 * rows * cols * BLOCK, bytes_accessed=4 * rows * cols, transcendentals=0),
        name='split_columns',
    )(w)


def pick_kernel(slot_ref, tok_ref, out_ref):
    experts, _, capacity, _ = out_ref.shape
    lanes = lax.broadcasted_iota(jnp.int32, (capacity, tok_ref.shape[1]), 0)
    picks = jnp.concatenate([(lanes == slot_ref[0, e:e + 1, :]).astype(jnp.float32) for e in range(experts)], axis=0).astype(jnp.bfloat16)
    for n in range(0, tok_ref.shape[2], 512):
        rows = jnp.dot(picks, tok_ref[0, :, n:n + 512], preferred_element_type=jnp.float32).astype(jnp.bfloat16)
        for e in range(experts):
            out_ref[e, 0, :, n:n + 512] = rows[e * capacity:(e + 1) * capacity]


def pick_rows(slot, tokens, capacity):
    sources, experts, tok_dev = slot.shape
    d_model = tokens.shape[2]
    return pl.pallas_call(
        pick_kernel,
        grid=(sources,),
        in_specs=[pl.BlockSpec((1, experts, tok_dev), lambda i: (i, 0, 0)), pl.BlockSpec((1, tok_dev, d_model), lambda i: (i, 0, 0))],
        out_specs=pl.BlockSpec((experts, 1, capacity, d_model), lambda i: (0, i, 0, 0)),
        out_shape=jax.ShapeDtypeStruct((experts, sources, capacity, d_model), jnp.bfloat16),
        cost_estimate=pl.CostEstimate(flops=2 * sources * experts * capacity * tok_dev * d_model, bytes_accessed=2 * sources * d_model * (tok_dev + experts * capacity), transcendentals=0),
        name='pick_rows',
    )(slot, tokens)


def gate_up_kernel(x_ref, *refs, jobs):
    w_refs, bias_refs, out_refs = refs[:jobs], refs[jobs:2 * jobs], refs[2 * jobs:]
    steps = pl.num_programs(0) // jobs
    for j in range(jobs):
        @pl.when(pl.program_id(0) // steps == j)
        def _():
            perm = even_odd(jnp.bfloat16)
            bias = jnp.broadcast_to(bias_refs[j][...].astype(jnp.float32), (16, BLOCK)).astype(jnp.bfloat16)
            bias = jnp.dot(bias, perm, preferred_element_type=jnp.float32)[0:1]
            u = jnp.dot(x_ref[0], w_refs[j][...], preferred_element_type=jnp.float32)
            u = (u + bias).astype(jnp.bfloat16).astype(jnp.float32)
            gate = jnp.minimum(u[:, :HALF], LIMIT)
            linear = jnp.clip(u[:, HALF:], -LIMIT, LIMIT)
            out_refs[j][...] = (gate * jax.nn.sigmoid(ALPHA * gate) * (linear + 1.0)).astype(jnp.bfloat16)


def gate_up(rows, jobs):
    total, d_model = rows.shape[1:]
    steps = jobs[0][2].shape[1] // BLOCK

    def block(j, i):
        return jnp.clip(i - j * steps, 0, steps - 1)

    def expert(i):
        return sum(jnp.where(i // steps == j, job[0], 0) for j, job in enumerate(jobs))

    count = len(jobs)
    return pl.pallas_call(
        functools.partial(gate_up_kernel, jobs=count),
        grid=(count * steps,),
        in_specs=[pl.BlockSpec((1, total, d_model), lambda i: (expert(i), 0, 0))]
        + [pl.BlockSpec((d_model, BLOCK), lambda i, j=j: (0, block(j, i))) for j in range(count)]
        + [pl.BlockSpec((1, BLOCK), lambda i, j=j: (0, jobs[j][1] * steps + block(j, i))) for j in range(count)],
        out_specs=[pl.BlockSpec((total, HALF), lambda i, j=j: (0, block(j, i))) for j in range(count)],
        out_shape=[jax.ShapeDtypeStruct((total, steps * HALF), jnp.bfloat16)] * count,
        cost_estimate=pl.CostEstimate(flops=2 * count * total * jobs[0][2].size, bytes_accessed=2 * count * (jobs[0][2].size + total * d_model), transcendentals=0),
        name='gate_up',
    )(rows, *[job[2] for job in jobs], *[job[3] for job in jobs])


def down_kernel(*refs, jobs):
    ins, out_refs = refs[:4 * jobs], refs[4 * jobs:]
    steps = pl.num_programs(0) // jobs
    for j in range(jobs):
        z0_ref, z1_ref, w_ref, bias_ref = ins[4 * j:4 * j + 4]

        @pl.when(pl.program_id(0) // steps == j)
        def _():
            z = jnp.concatenate([z0_ref[...], z1_ref[...]], axis=1)
            y = jnp.dot(z, w_ref[...], preferred_element_type=jnp.float32)
            out_refs[j][...] = (y + bias_ref[...].astype(jnp.float32)).astype(jnp.bfloat16)


def down(jobs):
    total, half_ff = jobs[0][0].shape
    d_ff, d_model = jobs[0][2].shape
    tile = 512
    steps, first, count = d_model // tile, 2 * d_ff // tile, len(jobs)

    def block(j, i):
        return jnp.clip(i - j * steps, 0, steps - 1)

    in_specs = []
    for j in range(count):
        in_specs += [pl.BlockSpec((total, half_ff), lambda i: (0, 0))] * 2
        in_specs += [pl.BlockSpec((d_ff, tile), lambda i, j=j: (0, block(j, i))), pl.BlockSpec((1, tile), lambda i, j=j: (0, first + block(j, i)))]
    return pl.pallas_call(
        functools.partial(down_kernel, jobs=count),
        grid=(count * steps,),
        in_specs=in_specs,
        out_specs=[pl.BlockSpec((total, tile), lambda i, j=j: (0, block(j, i))) for j in range(count)],
        out_shape=[jax.ShapeDtypeStruct((total, d_model), jnp.bfloat16)] * count,
        cost_estimate=pl.CostEstimate(flops=2 * count * total * d_ff * d_model, bytes_accessed=2 * count * (d_ff * d_model + total * d_model), transcendentals=0),
        name='down',
    )(*[a for job in jobs for a in job])


def gate_terms(slot, gate, experts, capacity):
    lanes = lax.broadcasted_iota(jnp.int32, (capacity, slot.shape[1]), 0)
    spread = jnp.concatenate([jnp.where(lanes == slot[e:e + 1, :], gate[e:e + 1, :], 0.0) for e in experts], axis=0).T
    high = spread.astype(jnp.bfloat16)
    rest = spread - high.astype(jnp.float32)
    mid = rest.astype(jnp.bfloat16)
    low = (rest - mid.astype(jnp.float32)).astype(jnp.bfloat16)
    return jnp.concatenate([low, mid, high], axis=1)


def early_kernel(slot_ref, gate_ref, *refs, experts):
    *y_refs, out_ref, y_all = refs
    capacity = y_refs[0].shape[1]
    count = len(experts) * capacity
    for i in range(len(experts)):
        for term in range(3):
            y_all[term * count + i * capacity:term * count + (i + 1) * capacity, :] = y_refs[i][0]
    terms = gate_terms(slot_ref[0], gate_ref[0], experts, capacity)
    for n in range(0, y_all.shape[1], 512):
        out_ref[:, n:n + 512] = jnp.dot(terms, y_all[:, n:n + 512], preferred_element_type=jnp.float32)


def early_sum(slot, gate, ys, experts):
    sources, count, tok_dev = slot.shape
    capacity, d_model = ys[0].shape[0] // sources, ys[0].shape[1]
    return pl.pallas_call(
        functools.partial(early_kernel, experts=experts),
        grid=(sources,),
        in_specs=[pl.BlockSpec((1, count, tok_dev), lambda i: (i, 0, 0))] * 2 + [pl.BlockSpec((1, capacity, d_model), lambda i: (i, 0, 0))] * len(ys),
        out_specs=pl.BlockSpec((tok_dev, d_model), lambda i: (i, 0)),
        out_shape=jax.ShapeDtypeStruct((sources * tok_dev, d_model), jnp.float32),
        scratch_shapes=[pltpu.VMEM((3 * len(ys) * capacity, d_model), jnp.bfloat16)],
        cost_estimate=pl.CostEstimate(flops=6 * sources * tok_dev * len(ys) * capacity * d_model, bytes_accessed=sources * d_model * (2 * len(ys) * capacity + 4 * tok_dev), transcendentals=0),
        name='early_sum',
    )(slot, gate, *[y.reshape(sources, capacity, d_model) for y in ys])


def late_kernel(slot_ref, gate_ref, za0, za1, zb0, zb1, wa0, wa1, wb0, wb1, bias_a, bias_b, old_ref, out_ref, y_all, w_all, *, experts):
    group, capacity = GROUP, za0.shape[0] // (2 * GROUP)
    tok_dev = slot_ref.shape[2]
    d_model = out_ref.shape[1]
    first = bias_a.shape[1] - d_model
    count = len(experts) * capacity
    part = lax.rem(pl.program_id(0), 2)

    half_ff = wa0.shape[0]

    @pl.when(pl.program_id(0) == 0)
    def _():
        for i, (w0, w1) in enumerate(((wa0, wa1), (wb0, wb1))):
            w_all[i, :half_ff] = w0[...]
            w_all[i, half_ff:] = w1[...]

    @pl.when(part == 0)
    def _():
        for i, (z0, z1, bias) in enumerate(((za0, za1, bias_a), (zb0, zb1, bias_b))):
            z = jnp.concatenate([z0[...], z1[...]], axis=1)
            for n in range(0, d_model, 512):
                y = jnp.dot(z, w_all[i, :, n:n + 512], preferred_element_type=jnp.float32)
                y = (y + bias[:, first + n:first + n + 512].astype(jnp.float32)).astype(jnp.bfloat16)
                for s in range(2 * group):
                    for term in range(3):
                        y_all[s, term * count + i * capacity:term * count + (i + 1) * capacity, n:n + 512] = y[s * capacity:(s + 1) * capacity]

    for s in range(group):
        terms = gate_terms(slot_ref[s], gate_ref[s], experts, capacity)
        for n in range(0, d_model, 512):
            rows = pl.ds(s * tok_dev, tok_dev)
            out_ref[rows, n:n + 512] = old_ref[rows, n:n + 512] + jnp.dot(terms, y_all[part * group + s, :, n:n + 512], preferred_element_type=jnp.float32)


def late_sum(slot, gate, zs, weights, biases, experts, old):
    sources, count, tok_dev = slot.shape
    total, half_ff = zs[0].shape
    d_model = old.shape[1]
    capacity = total // sources
    whole = lambda a: pl.BlockSpec(a.shape, lambda i: (0, 0))
    return pl.pallas_call(
        functools.partial(late_kernel, experts=experts),
        grid=(sources // GROUP,),
        in_specs=[pl.BlockSpec((GROUP, count, tok_dev), lambda i: (i, 0, 0))] * 2
        + [pl.BlockSpec((2 * GROUP * capacity, half_ff), lambda i: (i // 2, 0))] * 4
        + [whole(w) for w in weights] + [whole(b) for b in biases]
        + [pl.BlockSpec((GROUP * tok_dev, d_model), lambda i: (i, 0))],
        out_specs=pl.BlockSpec((GROUP * tok_dev, d_model), lambda i: (i, 0)),
        out_shape=jax.ShapeDtypeStruct(old.shape, jnp.float32),
        scratch_shapes=[pltpu.VMEM((2 * GROUP, 3 * len(experts) * capacity, d_model), jnp.bfloat16), pltpu.VMEM((len(experts), 2 * half_ff, d_model), jnp.bfloat16)],
        cost_estimate=pl.CostEstimate(flops=2 * total * 4 * half_ff * d_model + 6 * old.size * len(experts) * capacity, bytes_accessed=8 * old.size, transcendentals=0),
        name='late_sum',
    )(slot, gate, *zs, *weights, *biases, old)


def solution(mesh):
    torus = Mesh(mesh.devices.reshape(4, 4, 4, 2), ALL)
    rows_spec = P(ALL, None)
    plus = [(i, (i + 1) % 4) for i in range(4)]
    minus = [(i, (i + 3) % 4) for i in range(4)]
    swap = [(0, 1), (1, 0)]

    def local_block(x_in, expert_ids, norm_weight, router_w, router_b, w_gate_up, b_gate_up, w_down, b_down):
        tok_dev, d_model = x_in.shape
        top_k = expert_ids.shape[1]
        capacity = CAPACITY_FACTOR * top_k * tok_dev // 128
        d_ff = w_down.shape[1]
        zi, yi, xi, ci = (lax.axis_index(a) for a in ALL)
        first = (zi * 4 + yi) * 8

        gu0, gu1 = split_columns(w_gate_up)
        own = dict(wd=w_down[0], gu0=gu0, gu1=gu1, b=jnp.concatenate([b_gate_up, b_down], axis=1))
        left = {k: lax.ppermute(w, 'x', plus) for k, w in own.items()}
        right = {k: lax.ppermute(w, 'x', minus) for k, w in own.items()}
        far = dict(
            gu0=lax.ppermute(left['gu0'], 'x', plus),
            gu1=lax.ppermute(right['gu1'], 'x', minus),
            wd0=lax.ppermute(left['wd'][:d_ff // 2], 'x', plus),
            wd1=lax.ppermute(right['wd'][d_ff // 2:], 'x', minus),
            b=lax.ppermute(left['b'], 'x', plus),
        )
        sets = [(0, own), (3, left), (1, right), (2, far)]

        hidden = rms_norm(x_in, norm_weight)
        tokens = lax.all_gather(hidden, RING, axis=0, tiled=False).reshape(16, tok_dev, d_model)
        gates = route_gates(hidden, expert_ids, router_w, router_b)
        info = lax.all_gather(jnp.concatenate([expert_ids.T.astype(jnp.float32), gates.T], axis=0), RING, axis=0, tiled=False).reshape(16, 2 * top_k, tok_dev)
        ids, gates = info[:, :top_k].astype(jnp.int32), info[:, top_k:]

        experts = first + jnp.stack([((xi + step) % 4) * 2 + (ci if same else 1 - ci) for step, _ in sets for same in (True, False)])
        match = ids[:, None, :, :] == experts[None, :, None, None]
        member = jnp.any(match, axis=2)
        gate = jnp.sum(jnp.where(match, gates[:, None, :, :], 0.0), axis=2)
        before = (jnp.arange(tok_dev)[:, None] < jnp.arange(tok_dev)[None, :]).astype(jnp.bfloat16)
        rank = jnp.einsum('seu,ut->set', member.astype(jnp.bfloat16), before, preferred_element_type=jnp.float32).astype(jnp.int32)
        slot = jnp.where(member, rank, -1)

        rows = pick_rows(slot, tokens, capacity).reshape(8, 16 * capacity, d_model)
        held = []
        for _, weights in sets:
            held += [weights, {k: lax.ppermute(w, 'c', swap) for k, w in weights.items()}]
        z = {}
        for jobs in GATE_JOBS.values():
            done = gate_up(rows, [(e, i, held[e]['gu%d' % i], held[e]['b']) for e, i in jobs])
            z.update(zip(jobs, done))
        ys = {}
        for jobs in DOWN_JOBS.values():
            ys.update(zip(jobs, down([(z[e, 0], z[e, 1], held[e]['wd'], held[e]['b']) for e in jobs])))
        ys = [ys[e] for e in range(6)]
        last = [z[e, i] for e in (6, 7) for i in (0, 1)]
        early = early_sum(slot, gate, ys, range(6))
        total = late_sum(slot, gate, last, [held[e]['wd%d' % i] for e in (6, 7) for i in (0, 1)], [held[6]['b'], held[7]['b']], range(6, 8), early)
        mixed = lax.psum_scatter(total, RING, scatter_dimension=0, tiled=True)
        return (x_in.astype(jnp.float32) + mixed).astype(jnp.bfloat16)

    w3, w2 = P(ALL, None, None), P(ALL, None)
    return jax.shard_map(local_block, mesh=torus, in_specs=(rows_spec, rows_spec, P(), P(), P(), w3, w2, w3, w2), out_specs=rows_spec, check_vma=False)
```

profile of v0, /device:TPU:63, one launch (start us, length us, event | category | flops | bytes accessed | tf_op | source)
XLA Modules:
  0.0 773.1 jit_solution(15093848261512888870)
XLA Ops:
  8.8 2.5 fusion.2
  11.4 6.7 split_columns.1
  23.0 132.2 %collective-permute-done.6.refs_4_.refs_3_ = bf16[1,3584]{1,0:T(2,128)(2,1)S(1)} collective-permute-done((bf16[1,3584]{1,0:T(2,128)(2,1)S(1)}, bf16[1,3584]{1,0:T(2,128)(2,1)S(1)}, u32[]{:S(2)}, u32[]{:S(2)}) %collective-permute-start.6) | collective-permute-done | bytes 7200 | tf_op jit(solution)/shard_map/ppermute | solution.py:281
  155.7 2.1 collective-permute-start.7
  159.0 2.6 collective-permute-start.22
  165.9 2.7 collective-permute-start.1
  168.6 65.2 %collective-permute-done.11.refs_6_ = bf16[768,2048]{1,0:T(8,128)(2,1)} collective-permute-done((bf16[768,2048]{1,0:T(8,128)(2,1)}, bf16[768,2048]{1,0:T(8,128)(2,1)}, u32[]{:S(2)}, u32[]{:S(2)}) %collective-permute-start.11) | collective-permute-done | bytes 3145760 | tf_op jit(solution)/shard_map/ppermute | solution.py:282
  237.5 63.6 %collective-permute-done.25.refs_1_ = bf16[2048,768]{1,0:T(8,128)(2,1)} collective-permute-done((bf16[2048,768]{1,0:T(8,128)(2,1)}, bf16[2048,768]{1,0:T(8,128)(2,1)}, u32[]{:S(2)}, u32[]{:S(2)}) %collective-permute-start.25) | collective-permute-done | bytes 3145760 | tf_op jit(solution)/shard_map/ppermute | solution.py:282
  302.9 19.4 %all-gather = f32[256,256]{1,0:T(8,128)S(1)} all-gather(f32[16,256]{1,0:T(8,128)S(1)} %pad_maximum_fusion), channel_id=2, replica_groups=mesh['z'=4,'y'=4,'x'=4,'c'=2] {'z','y'}, dimensions={0}, use_global_device_ids=true | all-gather | bytes 278528 | tf_op jit(solution)/shard_map/all_gather | solution.py:295
  324.6 2.8 slice.18
  329.0 3.8 collective-permute-start.16
  333.4 23.9 %pick_rows.1 = bf16[8,16,64,2048]{3,2,1,0:T(8,128)(2,1)} custom-call(s32[16,8,256]{2,1,0:T(8,128)} %fusion.4.slot_ref, bf16[16,256,2048]{2,1,0:T(8,128)(2,1)} %bitcast.32), custom_call_target="tpu_custom_call" | custom-call | flops 8589934592 | bytes 50331648 | tf_op jit(solution)/shard_map/pick_rows/pallas_call | solution.py:84
  357.3 24.4 %gate_up.6 = (bf16[1024,384]{1,0:T(8,128)(2,1)}, bf16[1024,384]{1,0:T(8,128)(2,1)}, bf16[1024,384]{1,0:T(8,128)(2,1)}, bf16[1024,384]{1,0:T(8,128)(2,1)}) custom-call(bf16[8,1024,2048]{2,1,0:T(8,128)(2,1)} %bitcast.28, bf16[2048,768]{1,0:T(8,128)(2,1)} %collective-permute-done.refs_0_, bf16[2048,768]{1,0:T(8,128)(2,1)} %collective-permute-done.2.refs_1_, ...), custom_call_target="tpu_custom_call" | custom-call | flops 12884901888 | bytes 29360128 | tf_op jit(solution)/shard_map/gate_up/pallas_call | solution.py:122
  381.7 2.1 collective-permute-start.10
  384.6 24.5 %gate_up.7 = (bf16[1024,384]{1,0:T(8,128)(2,1)}, bf16[1024,384]{1,0:T(8,128)(2,1)}, bf16[1024,384]{1,0:T(8,128)(2,1)}, bf16[1024,384]{1,0:T(8,128)(2,1)}) custom-call(bf16[8,1024,2048]{2,1,0:T(8,128)(2,1)} %bitcast.29, bf16[2048,768]{1,0:T(8,128)(2,1)} %collective-permute-done.24.refs_0_, bf16[2048,768]{1,0:T(8,128)(2,1)} %collective-permute-done.25.refs_1_, ...), custom_call_target="tpu_custom_call" | custom-call | flops 12884901888 | bytes 29360128 | tf_op jit(solution)/shard_map/gate_up/pallas_call | solution.py:122
  409.8 13.1 %down.4 = (bf16[1024,2048]{1,0:T(8,128)(2,1)}, bf16[1024,2048]{1,0:T(8,128)(2,1)}) custom-call(bf16[1024,384]{1,0:T(8,128)(2,1)} %get-tuple-element.41.refs_0_, bf16[1024,384]{1,0:T(8,128)(2,1)} %get-tuple-element.42.refs_1_, bf16[768,2048]{1,0:T(8,128)(2,1)} %collective-permute-done.9.refs_2_, bf16[1,3584]{1,0:T(2,128)(2,1)} %copy-done.14, ...), custom_call_target="tpu_custom_call" | custom-call | flops 6442450944 | bytes 14680064 | tf_op jit(solution)/shard_map/down/pallas_call | solution.py:161
  423.0 23.3 %gate_up.5 = (bf16[1024,384]{1,0:T(8,128)(2,1)}, bf16[1024,384]{1,0:T(8,128)(2,1)}, bf16[1024,384]{1,0:T(8,128)(2,1)}, bf16[1024,384]{1,0:T(8,128)(2,1)}) custom-call(bf16[8,1024,2048]{2,1,0:T(8,128)(2,1)} %bitcast.30, bf16[2048,768]{1,0:T(8,128)(2,1)} %get-tuple-element.29.refs_0_, bf16[2048,768]{1,0:T(8,128)(2,1)} %get-tuple-element.30.refs_1_, ...), custom_call_target="tpu_custom_call" | custom-call | flops 12884901888 | bytes 29360128 | tf_op jit(solution)/shard_map/gate_up/pallas_call | solution.py:122
  446.3 13.2 %down.3 = (bf16[1024,2048]{1,0:T(8,128)(2,1)}, bf16[1024,2048]{1,0:T(8,128)(2,1)}) custom-call(bf16[1024,384]{1,0:T(8,128)(2,1)} %get-tuple-element.35.refs_0_, bf16[1024,384]{1,0:T(8,128)(2,1)} %get-tuple-element.36.refs_1_, bf16[768,2048]{1,0:T(8,128)(2,1)} %bitcast.14.refs_2_, bf16[1,3584]{1,0:T(2,128)(2,1)} %copy-done.10, ...), custom_call_target="tpu_custom_call" | custom-call | flops 6442450944 | bytes 14680064 | tf_op jit(solution)/shard_map/down/pallas_call | solution.py:161
  461.4 23.5 %gate_up.4 = (bf16[1024,384]{1,0:T(8,128)(2,1)}, bf16[1024,384]{1,0:T(8,128)(2,1)}, bf16[1024,384]{1,0:T(8,128)(2,1)}, bf16[1024,384]{1,0:T(8,128)(2,1)}) custom-call(bf16[8,1024,2048]{2,1,0:T(8,128)(2,1)} %bitcast.31, bf16[2048,768]{1,0:T(8,128)(2,1)} %collective-permute-done.1.refs_0_, bf16[2048,768]{1,0:T(8,128)(2,1)} %collective-permute-done.3.refs_1_, ...), custom_call_target="tpu_custom_call" | custom-call | flops 12884901888 | bytes 29360128 | tf_op jit(solution)/shard_map/gate_up/pallas_call | solution.py:122
  484.8 13.1 %down.5 = (bf16[1024,2048]{1,0:T(8,128)(2,1)}, bf16[1024,2048]{1,0:T(8,128)(2,1)}) custom-call(bf16[1024,384]{1,0:T(8,128)(2,1)} %get-tuple-element.46.refs_0_, bf16[1024,384]{1,0:T(8,128)(2,1)} %get-tuple-element.47.refs_1_, bf16[768,2048]{1,0:T(8,128)(2,1)} %collective-permute-done.28.refs_2_, bf16[1,3584]{1,0:T(2,128)(2,1)} %copy-done.11, ...), custom_call_target="tpu_custom_call" | custom-call | flops 6442450944 | bytes 14680064 | tf_op jit(solution)/shard_map/down/pallas_call | solution.py:161
  498.0 32.4 %early_sum.1.old_ref = f32[4096,2048]{1,0:T(8,128)} custom-call(s32[16,8,256]{2,1,0:T(8,128)} %fusion.4.slot_ref, f32[16,8,256]{2,1,0:T(8,128)} %fusion.5.gate_ref, bf16[16,64,2048]{2,1,0:T(8,128)(2,1)} %bitcast.36, bf16[16,64,2048]{2,1,0:T(8,128)(2,1)} %bitcast.37, bf16[16,64,2048]{2,1,0:T(8,128)(2,1)} %bitcast.34, bf16[16,64,2048]{2,1,0:T(8,128)(2,1)} %bitcast.38, ...), custom_call_target="tpu_custom_call" | custom-call | flops 19327352832 | bytes 58720256 | tf_op jit(solution)/shard_map/early_sum/pallas_call | solution.py:197
  531.6 37.2 %late_sum.1 = f32[4096,2048]{1,0:T(8,128)} custom-call(s32[16,8,256]{2,1,0:T(8,128)} %fusion.4.slot_ref, f32[16,8,256]{2,1,0:T(8,128)} %fusion.5.gate_ref, bf16[1024,384]{1,0:T(8,128)(2,1)} %get-tuple-element.31.za0, bf16[1024,384]{1,0:T(8,128)(2,1)} %get-tuple-element.32.za1, bf16[1024,384]{1,0:T(8,128)(2,1)} %get-tuple-element.33.zb0, ...), custom_call_target="tpu_custom_call" | custom-call | flops 12884901888 | bytes 67108864 | tf_op jit(solution)/shard_map/late_sum/pallas_call | solution.py:249
  568.9 194.3 %reduce-scatter.2.cloned.1.call-done = f32[256,2048]{1,0:T(8,128)} async-done(((f32[4096,2048]{1,0:T(8,128)}), f32[256,2048]{1,0:T(8,128)}) %reduce-scatter.2.cloned.1.call-update) | async-done | bytes 2097168 | tf_op jit(solution)/shard_map/reduce_scatter | solution.py:321
  763.2 2.8 fusion.3
  (113 shorter events, 27.6 us)
Async XLA Ops:
  6.5 326.8 %all-gather.4.cloned.1.call-start = ((), (), s32[]{:S(2)}) async-start(), calls=%async_computation.2 | async-start | bytes 17825792 | tf_op jit(solution)/shard_map/all_gather | solution.py:293
  11.4 751.8 %reduce-scatter.2.cloned.1.call-start = ((), (), s32[]{:S(2)}) async-start(), calls=%async_computation.1 | async-start | bytes 35651584 | tf_op jit(solution)/shard_map/reduce_scatter | solution.py:321
  18.2 145.7 %collective-permute-start = (bf16[2048,768]{1,0:T(8,128)(2,1)}, bf16[2048,768]{1,0:T(8,128)(2,1)}, u32[]{:S(2)}, u32[]{:S(2)}) collective-permute-start(bf16[2048,768]{1,0:T(8,128)(2,1)} %get-tuple-element.29.refs_0_), channel_id=1, source_target_pairs={{0,2},{2,4},{4,6},{6,0},{1,3},{3,5},{5,7},{7,1},{8,10},{10,12},{12... | collective-permute-start | bytes 9437192 | tf_op jit(solution)/shard_map/ppermute | solution.py:281
  18.4 147.5 %collective-permute-start.2 = (bf16[2048,768]{1,0:T(8,128)(2,1)}, bf16[2048,768]{1,0:T(8,128)(2,1)}, u32[]{:S(2)}, u32[]{:S(2)}) collective-permute-start(bf16[2048,768]{1,0:T(8,128)(2,1)} %get-tuple-element.30.refs_1_), channel_id=1, source_target_pairs={{0,6},{2,0},{4,2},{6,4},{1,7},{3,1},{5,3},{7,5},{8,14},{10,8},{12,... | collective-permute-start | bytes 9437192 | tf_op jit(solution)/shard_map/ppermute | solution.py:282
  19.6 146.2 %collective-permute-start.9 = (bf16[768,2048]{1,0:T(8,128)(2,1)}, bf16[768,2048]{1,0:T(8,128)(2,1)}, u32[]{:S(2)}, u32[]{:S(2)}) collective-permute-start(bf16[768,2048]{1,0:T(8,128)(2,1)} %bitcast.14.refs_2_), channel_id=1, source_target_pairs={{0,2},{2,4},{4,6},{6,0},{1,3},{3,5},{5,7},{7,1},{8,10},{10,12},{12... | collective-permute-start | bytes 9437192 | tf_op jit(solution)/shard_map/ppermute | solution.py:281
  21.1 134.1 %collective-permute-start.6 = (bf16[1,3584]{1,0:T(2,128)(2,1)S(1)}, bf16[1,3584]{1,0:T(2,128)(2,1)S(1)}, u32[]{:S(2)}, u32[]{:S(2)}) collective-permute-start(bf16[1,3584]{1,0:T(2,128)(2,1)S(1)} %constant_dynamic-update-slice_fusion.refs_4_.refs_5_.refs_3_), channel_id=1, source_target_pairs={{0,2},{2,4},{4,6},{6,0},{1,3},{3,5},{5,7},{7,1},{8,10},{10,12},{12... | collective-permute-start | bytes 21512 | tf_op jit(solution)/shard_map/ppermute | solution.py:281
  21.2 134.6 %collective-permute-start.17 = (bf16[1,3584]{1,0:T(2,128)(2,1)S(1)}, bf16[1,3584]{1,0:T(2,128)(2,1)S(1)}, u32[]{:S(2)}, u32[]{:S(2)}) collective-permute-start(bf16[1,3584]{1,0:T(2,128)(2,1)S(1)} %constant_dynamic-update-slice_fusion.refs_4_.refs_5_.refs_3_), channel_id=1, source_target_pairs={{0,1},{1,0},{2,3},{3,2},{4,5},{5,4},{6,7},{7,6},{8,9},{9,8},{10,11... | collective-permute-start | bytes 21512 | tf_op jit(solution)/shard_map/ppermute | solution.py:309
  162.7 71.0 %collective-permute-start.11 = (bf16[768,2048]{1,0:T(8,128)(2,1)}, bf16[768,2048]{1,0:T(8,128)(2,1)}, u32[]{:S(2)}, u32[]{:S(2)}) collective-permute-start(bf16[768,2048]{1,0:T(8,128)(2,1)} %bitcast.14.refs_2_), channel_id=1, source_target_pairs={{0,6},{2,0},{4,2},{6,4},{1,7},{3,1},{5,3},{7,5},{8,14},{10,8},{12,... | collective-permute-start | bytes 9437192 | tf_op jit(solution)/shard_map/ppermute | solution.py:282
  163.6 71.8 %collective-permute-start.15 = (bf16[2048,768]{1,0:T(8,128)(2,1)}, bf16[2048,768]{1,0:T(8,128)(2,1)}, u32[]{:S(2)}, u32[]{:S(2)}) collective-permute-start(bf16[2048,768]{1,0:T(8,128)(2,1)} %get-tuple-element.29.refs_0_), channel_id=1, source_target_pairs={{0,1},{1,0},{2,3},{3,2},{4,5},{5,4},{6,7},{7,6},{8,9},{9,8},{10,11... | collective-permute-start | bytes 9437192 | tf_op jit(solution)/shard_map/ppermute | solution.py:309
  163.9 73.5 %collective-permute-start.24 = (bf16[2048,768]{1,0:T(8,128)(2,1)}, bf16[2048,768]{1,0:T(8,128)(2,1)}, u32[]{:S(2)}, u32[]{:S(2)}) collective-permute-start(bf16[2048,768]{1,0:T(8,128)(2,1)} %get-tuple-element.30.refs_1_), channel_id=1, source_target_pairs={{0,2},{2,4},{4,6},{6,0},{1,3},{3,5},{5,7},{7,1},{8,10},{10,12},{12... | collective-permute-start | bytes 9437192 | tf_op jit(solution)/shard_map/ppermute | solution.py:281
  165.9 135.3 %collective-permute-start.25 = (bf16[2048,768]{1,0:T(8,128)(2,1)}, bf16[2048,768]{1,0:T(8,128)(2,1)}, u32[]{:S(2)}, u32[]{:S(2)}) collective-permute-start(bf16[2048,768]{1,0:T(8,128)(2,1)} %get-tuple-element.29.refs_0_), channel_id=1, source_target_pairs={{0,6},{2,0},{4,2},{6,4},{1,7},{3,1},{5,3},{7,5},{8,14},{10,8},{12,... | collective-permute-start | bytes 9437192 | tf_op jit(solution)/shard_map/ppermute | solution.py:282
  165.9 136.9 %collective-permute-start.1 = (bf16[2048,768]{1,0:T(8,128)(2,1)}, bf16[2048,768]{1,0:T(8,128)(2,1)}, u32[]{:S(2)}, u32[]{:S(2)}) collective-permute-start(bf16[2048,768]{1,0:T(8,128)(2,1)} %collective-permute-done.refs_0_), channel_id=1, source_target_pairs={{0,2},{2,4},{4,6},{6,0},{1,3},{3,5},{5,7},{7,1},{8,10},{10,12},{12... | collective-permute-start | bytes 9437192 | tf_op jit(solution)/shard_map/ppermute | solution.py:284
  233.8 95.2 %collective-permute-start.19 = (bf16[2048,768]{1,0:T(8,128)(2,1)}, bf16[2048,768]{1,0:T(8,128)(2,1)}, u32[]{:S(2)}, u32[]{:S(2)}) collective-permute-start(bf16[2048,768]{1,0:T(8,128)(2,1)} %collective-permute-done.refs_0_), channel_id=1, source_target_pairs={{0,1},{1,0},{2,3},{3,2},{4,5},{5,4},{6,7},{7,6},{8,9},{9,8},{10,11... | collective-permute-start | bytes 9437192 | tf_op jit(solution)/shard_map/ppermute | solution.py:309
  235.4 97.4 %collective-permute-start.20 = (bf16[2048,768]{1,0:T(8,128)(2,1)}, bf16[2048,768]{1,0:T(8,128)(2,1)}, u32[]{:S(2)}, u32[]{:S(2)}) collective-permute-start(bf16[2048,768]{1,0:T(8,128)(2,1)} %collective-permute-done.2.refs_1_), channel_id=1, source_target_pairs={{0,1},{1,0},{2,3},{3,2},{4,5},{5,4},{6,7},{7,6},{8,9},{9,8},{10,11... | collective-permute-start | bytes 9437192 | tf_op jit(solution)/shard_map/ppermute | solution.py:309
  237.4 144.3 %collective-permute-start.3 = (bf16[2048,768]{1,0:T(8,128)(2,1)}, bf16[2048,768]{1,0:T(8,128)(2,1)}, u32[]{:S(2)}, u32[]{:S(2)}) collective-permute-start(bf16[2048,768]{1,0:T(8,128)(2,1)} %collective-permute-done.2.refs_1_), channel_id=1, source_target_pairs={{0,6},{2,0},{4,2},{6,4},{1,7},{3,1},{5,3},{7,5},{8,14},{10,8},{12,... | collective-permute-start | bytes 9437192 | tf_op jit(solution)/shard_map/ppermute | solution.py:285
  301.2 82.6 %collective-permute-start.26 = (bf16[2048,768]{1,0:T(8,128)(2,1)}, bf16[2048,768]{1,0:T(8,128)(2,1)}, u32[]{:S(2)}, u32[]{:S(2)}) collective-permute-start(bf16[2048,768]{1,0:T(8,128)(2,1)} %collective-permute-done.24.refs_0_), channel_id=1, source_target_pairs={{0,1},{1,0},{2,3},{3,2},{4,5},{5,4},{6,7},{7,6},{8,9},{9,8},{10,11... | collective-permute-start | bytes 9437192 | tf_op jit(solution)/shard_map/ppermute | solution.py:309
  302.8 81.7 %collective-permute-start.27 = (bf16[2048,768]{1,0:T(8,128)(2,1)}, bf16[2048,768]{1,0:T(8,128)(2,1)}, u32[]{:S(2)}, u32[]{:S(2)}) collective-permute-start(bf16[2048,768]{1,0:T(8,128)(2,1)} %collective-permute-done.25.refs_1_), channel_id=1, source_target_pairs={{0,1},{1,0},{2,3},{3,2},{4,5},{5,4},{6,7},{7,6},{8,9},{9,8},{10,11... | collective-permute-start | bytes 9437192 | tf_op jit(solution)/shard_map/ppermute | solution.py:309
  329.0 80.1 %collective-permute-start.16 = (bf16[2048,768]{1,0:T(8,128)(2,1)}, bf16[2048,768]{1,0:T(8,128)(2,1)}, u32[]{:S(2)}, u32[]{:S(2)}) collective-permute-start(bf16[2048,768]{1,0:T(8,128)(2,1)} %get-tuple-element.30.refs_1_), channel_id=1, source_target_pairs={{0,1},{1,0},{2,3},{3,2},{4,5},{5,4},{6,7},{7,6},{8,9},{9,8},{10,11... | collective-permute-start | bytes 9437192 | tf_op jit(solution)/shard_map/ppermute | solution.py:309
  332.8 76.8 %collective-permute-start.18 = (bf16[768,2048]{1,0:T(8,128)(2,1)}, bf16[768,2048]{1,0:T(8,128)(2,1)}, u32[]{:S(2)}, u32[]{:S(2)}) collective-permute-start(bf16[768,2048]{1,0:T(8,128)(2,1)} %bitcast.14.refs_2_), channel_id=1, source_target_pairs={{0,1},{1,0},{2,3},{3,2},{4,5},{5,4},{6,7},{7,6},{8,9},{9,8},{10,11... | collective-permute-start | bytes 9437192 | tf_op jit(solution)/shard_map/ppermute | solution.py:309
  383.8 77.3 %collective-permute-start.4 = (bf16[2048,768]{1,0:T(8,128)(2,1)}, bf16[2048,768]{1,0:T(8,128)(2,1)}, u32[]{:S(2)}, u32[]{:S(2)}) collective-permute-start(bf16[2048,768]{1,0:T(8,128)(2,1)} %collective-permute-done.1.refs_0_), channel_id=1, source_target_pairs={{0,1},{1,0},{2,3},{3,2},{4,5},{5,4},{6,7},{7,6},{8,9},{9,8},{10,11... | collective-permute-start | bytes 9437192 | tf_op jit(solution)/shard_map/ppermute | solution.py:309
  384.5 76.9 %collective-permute-start.5 = (bf16[2048,768]{1,0:T(8,128)(2,1)}, bf16[2048,768]{1,0:T(8,128)(2,1)}, u32[]{:S(2)}, u32[]{:S(2)}) collective-permute-start(bf16[2048,768]{1,0:T(8,128)(2,1)} %collective-permute-done.3.refs_1_), channel_id=1, source_target_pairs={{0,1},{1,0},{2,3},{3,2},{4,5},{5,4},{6,7},{7,6},{8,9},{9,8},{10,11... | collective-permute-start | bytes 9437192 | tf_op jit(solution)/shard_map/ppermute | solution.py:309
  409.0 75.8 %collective-permute-start.28 = (bf16[768,2048]{1,0:T(8,128)(2,1)}, bf16[768,2048]{1,0:T(8,128)(2,1)}, u32[]{:S(2)}, u32[]{:S(2)}) collective-permute-start(bf16[768,2048]{1,0:T(8,128)(2,1)} %collective-permute-done.9.refs_2_), channel_id=1, source_target_pairs={{0,1},{1,0},{2,3},{3,2},{4,5},{5,4},{6,7},{7,6},{8,9},{9,8},{10,11... | collective-permute-start | bytes 9437192 | tf_op jit(solution)/shard_map/ppermute | solution.py:309
  409.6 75.3 %collective-permute-start.29 = (bf16[768,2048]{1,0:T(8,128)(2,1)}, bf16[768,2048]{1,0:T(8,128)(2,1)}, u32[]{:S(2)}, u32[]{:S(2)}) collective-permute-start(bf16[768,2048]{1,0:T(8,128)(2,1)} %collective-permute-done.11.refs_6_), channel_id=1, source_target_pairs={{0,1},{1,0},{2,3},{3,2},{4,5},{5,4},{6,7},{7,6},{8,9},{9,8},{10,11... | collective-permute-start | bytes 9437192 | tf_op jit(solution)/shard_map/ppermute | solution.py:309
  459.9 70.5 %collective-permute-start.13 = (bf16[384,2048]{1,0:T(8,128)(2,1)}, bf16[384,2048]{1,0:T(8,128)(2,1)S(1)}, u32[]{:S(2)}, u32[]{:S(2)}) collective-permute-start(bf16[384,2048]{1,0:T(8,128)(2,1)} %collective-permute-done.10.wa0), channel_id=1, source_target_pairs={{0,1},{1,0},{2,3},{3,2},{4,5},{5,4},{6,7},{7,6},{8,9},{9,8},{10,11... | collective-permute-start | bytes 4718600 | tf_op jit(solution)/shard_map/ppermute | solution.py:309
  (25 other events, 2953.9 us)
Sparse Core Ops, SparseCore 0:
  11.5 111.4 all-gather.3
  569.0 194.1 reduce-scatter.1
where the time goes:
time: 786 us; the launch traced here: 773 us
  waiting for transfers between devices  459 us (58%)
  Pallas kernels  235 us (30%)
  starting transfers between devices  28.3 us (4%)
  blocking collectives  19.4 us (2%)
  between operations  14 us (2%)
  other arithmetic  10.4 us (1%)
    reduce_scatter x1, waiting for transfers between devices, local_block(): mixed = lax.psum_scatter(total, RING, scatter_dimension=0, tiled=True)  194 us
    ppermute x4, waiting for transfers between devices, local_block(): left = {k: lax.ppermute(w, 'x', plus) for k, w in own.items()}  132 us
    ppermute x4, waiting for transfers between devices, local_block(): right = {k: lax.ppermute(w, 'x', minus) for k, w in own.items()}  130 us
    pallas_call x4, Pallas kernels, gate_up(): pl.pallas_call(functools.partial(gate_up_kernel, jobs=count), grid=(count...  95.6 us
    pallas_call x3, Pallas kernels, down(): pl.pallas_call(functools.partial(down_kernel, jobs=count), grid=(count *...  39.4 us
    pallas_call x1, Pallas kernels, late_sum(): pl.pallas_call(functools.partial(late_kernel, experts=experts), grid=(sou...  37.2 us
    pallas_call x1, Pallas kernels, early_sum(): pl.pallas_call(functools.partial(early_kernel, experts=experts), grid=(so...  32.4 us
    pallas_call x1, Pallas kernels, pick_rows(): pl.pallas_call(pick_kernel, grid=(sources,), in_specs=[pl.BlockSpec((1, e...  23.9 us
  transfers between devices with their start and end apart: 32, of which 8 were waited for; matrix products, arithmetic and copies ran while one was open for 1% of the time, Pallas kernels for 26%

commit v1 on v0

--- a/solution.py
+++ b/solution.py
@@ -19,7 +19,8 @@
     'za': ((0, 0), (0, 1), (1, 0), (1, 1)),
     'zb': ((2, 0), (4, 1), (3, 0), (5, 1)),
     'zc': ((2, 1), (4, 0), (3, 1), (5, 0)),
-    'zd': ((6, 0), (6, 1), (7, 0), (7, 1)),
+    'zd': ((6, 0), (6, 1)),
+    'ze': ((7, 0), (7, 1)),
 }
 DOWN_JOBS = {'ya': (0, 1), 'yb': (2, 4), 'yc': (3, 5)}
 RING = ('z', 'y')
@@ -69,13 +70,14 @@
 
 
 def pick_kernel(slot_ref, tok_ref, out_ref):
-    experts, _, capacity, _ = out_ref.shape
+    experts, sources, capacity, d_model = out_ref.shape
     lanes = lax.broadcasted_iota(jnp.int32, (capacity, tok_ref.shape[1]), 0)
-    picks = jnp.concatenate([(lanes == slot_ref[0, e:e + 1, :]).astype(jnp.float32) for e in range(experts)], axis=0).astype(jnp.bfloat16)
-    for n in range(0, tok_ref.shape[2], 512):
-        rows = jnp.dot(picks, tok_ref[0, :, n:n + 512], preferred_element_type=jnp.float32).astype(jnp.bfloat16)
-        for e in range(experts):
-            out_ref[e, 0, :, n:n + 512] = rows[e * capacity:(e + 1) * capacity]
+    for s in range(sources):
+        picks = jnp.concatenate([(lanes == slot_ref[s, e:e + 1, :]).astype(jnp.float32) for e in range(experts)], axis=0).astype(jnp.bfloat16)
+        for n in range(0, d_model, 512):
+            rows = jnp.dot(picks, tok_ref[s, :, n:n + 512], preferred_element_type=jnp.float32).astype(jnp.bfloat16)
+            for e in range(experts):
+                out_ref[e, s, :, n:n + 512] = rows[e * capacity:(e + 1) * capacity]
 
 
 def pick_rows(slot, tokens, capacity):
@@ -83,9 +85,9 @@
     d_model = tokens.shape[2]
     return pl.pallas_call(
         pick_kernel,
-        grid=(sources,),
-        in_specs=[pl.BlockSpec((1, experts, tok_dev), lambda i: (i, 0, 0)), pl.BlockSpec((1, tok_dev, d_model), lambda i: (i, 0, 0))],
-        out_specs=pl.BlockSpec((experts, 1, capacity, d_model), lambda i: (0, i, 0, 0)),
+        grid=(sources // GROUP,),
+        in_specs=[pl.BlockSpec((GROUP, experts, tok_dev), lambda i: (i, 0, 0)), pl.BlockSpec((GROUP, tok_dev, d_model), lambda i: (i, 0, 0))],
+        out_specs=pl.BlockSpec((experts, GROUP, capacity, d_model), lambda i: (0, i, 0, 0)),
         out_shape=jax.ShapeDtypeStruct((experts, sources, capacity, d_model), jnp.bfloat16),
         cost_estimate=pl.CostEstimate(flops=2 * sources * experts * capacity * tok_dev * d_model, bytes_accessed=2 * sources * d_model * (tok_dev + experts * capacity), transcendentals=0),
         name='pick_rows',
@@ -99,7 +101,7 @@
         @pl.when(pl.program_id(0) // steps == j)
         def _():
             perm = even_odd(jnp.bfloat16)
-            bias = jnp.broadcast_to(bias_refs[j][...].astype(jnp.float32), (16, BLOCK)).astype(jnp.bfloat16)
+            bias = jnp.broadcast_to(bias_refs[j][0].astype(jnp.float32), (16, BLOCK)).astype(jnp.bfloat16)
             bias = jnp.dot(bias, perm, preferred_element_type=jnp.float32)[0:1]
             u = jnp.dot(x_ref[0], w_refs[j][...], preferred_element_type=jnp.float32)
             u = (u + bias).astype(jnp.bfloat16).astype(jnp.float32)
@@ -124,7 +126,7 @@
         grid=(count * steps,),
         in_specs=[pl.BlockSpec((1, total, d_model), lambda i: (expert(i), 0, 0))]
         + [pl.BlockSpec((d_model, BLOCK), lambda i, j=j: (0, block(j, i))) for j in range(count)]
-        + [pl.BlockSpec((1, BLOCK), lambda i, j=j: (0, jobs[j][1] * steps + block(j, i))) for j in range(count)],
+        + [pl.BlockSpec((1, 1, BLOCK), lambda i, j=j: (jobs[j][0] % 2, 0, jobs[j][1] * steps + block(j, i))) for j in range(count)],
         out_specs=[pl.BlockSpec((total, HALF), lambda i, j=j: (0, block(j, i))) for j in range(count)],
         out_shape=[jax.ShapeDtypeStruct((total, steps * HALF), jnp.bfloat16)] * count,
         cost_estimate=pl.CostEstimate(flops=2 * count * total * jobs[0][2].size, bytes_accessed=2 * count * (jobs[0][2].size + total * d_model), transcendentals=0),
@@ -142,7 +144,7 @@
         def _():
             z = jnp.concatenate([z0_ref[...], z1_ref[...]], axis=1)
             y = jnp.dot(z, w_ref[...], preferred_element_type=jnp.float32)
-            out_refs[j][...] = (y + bias_ref[...].astype(jnp.float32)).astype(jnp.bfloat16)
+            out_refs[j][...] = (y + bias_ref[0].astype(jnp.float32)).astype(jnp.bfloat16)
 
 
 def down(jobs):
@@ -155,9 +157,10 @@
         return jnp.clip(i - j * steps, 0, steps - 1)
 
     in_specs = []
-    for j in range(count):
+    for j, job in enumerate(jobs):
+        which = job[4]
         in_specs += [pl.BlockSpec((total, half_ff), lambda i: (0, 0))] * 2
-        in_specs += [pl.BlockSpec((d_ff, tile), lambda i, j=j: (0, block(j, i))), pl.BlockSpec((1, tile), lambda i, j=j: (0, first + block(j, i)))]
+        in_specs += [pl.BlockSpec((d_ff, tile), lambda i, j=j: (0, block(j, i))), pl.BlockSpec((1, 1, tile), lambda i, j=j, which=which: (which, 0, first + block(j, i)))]
     return pl.pallas_call(
         functools.partial(down_kernel, jobs=count),
         grid=(count * steps,),
@@ -166,7 +169,7 @@
         out_shape=[jax.ShapeDtypeStruct((total, d_model), jnp.bfloat16)] * count,
         cost_estimate=pl.CostEstimate(flops=2 * count * total * d_ff * d_model, bytes_accessed=2 * count * (d_ff * d_model + total * d_model), transcendentals=0),
         name='down',
-    )(*[a for job in jobs for a in job])
+    )(*[a for job in jobs for a in job[:4]])
 
 
 def gate_terms(slot, gate, experts, capacity):
@@ -181,14 +184,16 @@
 
 def early_kernel(slot_ref, gate_ref, *refs, experts):
     *y_refs, out_ref, y_all = refs
-    capacity = y_refs[0].shape[1]
+    sources, capacity, d_model = y_refs[0].shape
+    tok_dev = slot_ref.shape[2]
     count = len(experts) * capacity
-    for i in range(len(experts)):
-        for term in range(3):
-            y_all[term * count + i * capacity:term * count + (i + 1) * capacity, :] = y_refs[i][0]
-    terms = gate_terms(slot_ref[0], gate_ref[0], experts, capacity)
-    for n in range(0, y_all.shape[1], 512):
-        out_ref[:, n:n + 512] = jnp.dot(terms, y_all[:, n:n + 512], preferred_element_type=jnp.float32)
+    for s in range(sources):
+        for i in range(len(experts)):
+            for term in range(3):
+                y_all[s, term * count + i * capacity:term * count + (i + 1) * capacity, :] = y_refs[i][s]
+        terms = gate_terms(slot_ref[s], gate_ref[s], experts, capacity)
+        for n in range(0, d_model, 512):
+            out_ref[s * tok_dev:(s + 1) * tok_dev, n:n + 512] = jnp.dot(terms, y_all[s, :, n:n + 512], preferred_element_type=jnp.float32)
 
 
 def early_sum(slot, gate, ys, experts):
@@ -196,11 +201,11 @@
     capacity, d_model = ys[0].shape[0] // sources, ys[0].shape[1]
     return pl.pallas_call(
         functools.partial(early_kernel, experts=experts),
-        grid=(sources,),
-        in_specs=[pl.BlockSpec((1, count, tok_dev), lambda i: (i, 0, 0))] * 2 + [pl.BlockSpec((1, capacity, d_model), lambda i: (i, 0, 0))] * len(ys),
-        out_specs=pl.BlockSpec((tok_dev, d_model), lambda i: (i, 0)),
+        grid=(sources // GROUP,),
+        in_specs=[pl.BlockSpec((GROUP, count, tok_dev), lambda i: (i, 0, 0))] * 2 + [pl.BlockSpec((GROUP, capacity, d_model), lambda i: (i, 0, 0))] * len(ys),
+        out_specs=pl.BlockSpec((GROUP * tok_dev, d_model), lambda i: (i, 0)),
         out_shape=jax.ShapeDtypeStruct((sources * tok_dev, d_model), jnp.float32),
-        scratch_shapes=[pltpu.VMEM((3 * len(ys) * capacity, d_model), jnp.bfloat16)],
+        scratch_shapes=[pltpu.VMEM((GROUP, 3 * len(ys) * capacity, d_model), jnp.bfloat16)],
         cost_estimate=pl.CostEstimate(flops=6 * sources * tok_dev * len(ys) * capacity * d_model, bytes_accessed=sources * d_model * (2 * len(ys) * capacity + 4 * tok_dev), transcendentals=0),
         name='early_sum',
     )(slot, gate, *[y.reshape(sources, capacity, d_model) for y in ys])
@@ -210,7 +215,7 @@
     group, capacity = GROUP, za0.shape[0] // (2 * GROUP)
     tok_dev = slot_ref.shape[2]
     d_model = out_ref.shape[1]
-    first = bias_a.shape[1] - d_model
+    first = bias_a.shape[2] - d_model
     count = len(experts) * capacity
     part = lax.rem(pl.program_id(0), 2)
 
@@ -228,7 +233,7 @@
             z = jnp.concatenate([z0[...], z1[...]], axis=1)
             for n in range(0, d_model, 512):
                 y = jnp.dot(z, w_all[i, :, n:n + 512], preferred_element_type=jnp.float32)
-                y = (y + bias[:, first + n:first + n + 512].astype(jnp.float32)).astype(jnp.bfloat16)
+                y = (y + bias[0, :, first + n:first + n + 512].astype(jnp.float32)).astype(jnp.bfloat16)
                 for s in range(2 * group):
                     for term in range(3):
                         y_all[s, term * count + i * capacity:term * count + (i + 1) * capacity, n:n + 512] = y[s * capacity:(s + 1) * capacity]
@@ -251,7 +256,7 @@
         grid=(sources // GROUP,),
         in_specs=[pl.BlockSpec((GROUP, count, tok_dev), lambda i: (i, 0, 0))] * 2
         + [pl.BlockSpec((2 * GROUP * capacity, half_ff), lambda i: (i // 2, 0))] * 4
-        + [whole(w) for w in weights] + [whole(b) for b in biases]
+        + [whole(w) for w in weights] + [pl.BlockSpec((1, 1, b.shape[2]), lambda i, which=which: (which, 0, 0)) for which, b in enumerate(biases)]
         + [pl.BlockSpec((GROUP * tok_dev, d_model), lambda i: (i, 0))],
         out_specs=pl.BlockSpec((GROUP * tok_dev, d_model), lambda i: (i, 0)),
         out_shape=jax.ShapeDtypeStruct(old.shape, jnp.float32),
@@ -277,7 +282,8 @@
         first = (zi * 4 + yi) * 8
 
         gu0, gu1 = split_columns(w_gate_up)
-        own = dict(wd=w_down[0], gu0=gu0, gu1=gu1, b=jnp.concatenate([b_gate_up, b_down], axis=1))
+        b_own = jnp.concatenate([b_gate_up, b_down], axis=1)
+        own = dict(wd=w_down[0], gu0=gu0, gu1=gu1, b=jnp.stack([b_own, lax.ppermute(b_own, 'c', swap)]))
         left = {k: lax.ppermute(w, 'x', plus) for k, w in own.items()}
         right = {k: lax.ppermute(w, 'x', minus) for k, w in own.items()}
         far = dict(
@@ -306,14 +312,14 @@
         rows = pick_rows(slot, tokens, capacity).reshape(8, 16 * capacity, d_model)
         held = []
         for _, weights in sets:
-            held += [weights, {k: lax.ppermute(w, 'c', swap) for k, w in weights.items()}]
+            held += [weights, {k: w if k == 'b' else lax.ppermute(w, 'c', swap) for k, w in weights.items()}]
         z = {}
         for jobs in GATE_JOBS.values():
             done = gate_up(rows, [(e, i, held[e]['gu%d' % i], held[e]['b']) for e, i in jobs])
             z.update(zip(jobs, done))
         ys = {}
         for jobs in DOWN_JOBS.values():
-            ys.update(zip(jobs, down([(z[e, 0], z[e, 1], held[e]['wd'], held[e]['b']) for e in jobs])))
+            ys.update(zip(jobs, down([(z[e, 0], z[e, 1], held[e]['wd'], held[e]['b'], e % 2) for e in jobs])))
         ys = [ys[e] for e in range(6)]
         last = [z[e, i] for e in (6, 7) for i in (0, 1)]
         early = early_sum(slot, gate, ys, range(6))

time: 786 us -> 784 us (level)
  starting transfers between devices: 28.3 us -> 47.8 us
  waiting for transfers between devices: 459 us -> 444 us
    ppermute x4, waiting for transfers between devices: 130 us -> 0.43 us  [local_block(): right = {k: lax.ppermute(w, 'x', minus) for k, w in own.items()}]
    ppermute x1, waiting for transfers between devices: 0.01 us -> 59.8 us  [local_block(): lax.ppermute(left['gu0'], 'x', plus)]
    ppermute x4, waiting for transfers between devices: 132 us -> 188 us  [local_block(): left = {k: lax.ppermute(w, 'x', plus) for k, w in own.items()}]
    ppermute x17 -> x13, starting transfers between devices: 15.8 us -> 33.7 us  [local_block(): lax.ppermute(w, 'c', swap)]
    pallas_call x4 -> x5, Pallas kernels: 95.6 us -> 96.8 us  [gate_up(): pl.pallas_call(functools.partial(gate_up_kernel, jobs=count), grid=(count...]
  transfers between devices with their start and end apart: 32 -> 29, of which waited for: 8 -> 8; matrix products, arithmetic and copies ran while one was open for 1% -> 1% of each run, Pallas kernels for 26% -> 25%
where the time goes in v1:
time: 784 us; the launch traced here: 772 us
  waiting for transfers between devices  444 us (57%)
  Pallas kernels  230 us (29%)
  starting transfers between devices  47.8 us (6%)
  blocking collectives  17.6 us (2%)
  between operations  14 us (2%)
  other arithmetic  10.4 us (1%)
    reduce_scatter x1, waiting for transfers between devices, local_block(): mixed = lax.psum_scatter(total, RING, scatter_dimension=0, tiled=True)  194 us
    ppermute x4, waiting for transfers between devices, local_block(): left = {k: lax.ppermute(w, 'x', plus) for k, w in own.items()}  188 us
    pallas_call x5, Pallas kernels, gate_up(): pl.pallas_call(functools.partial(gate_up_kernel, jobs=count), grid=(count...  96.8 us
    ppermute x1, waiting for transfers between devices, local_block(): lax.ppermute(left['gu0'], 'x', plus)  59.8 us
    pallas_call x3, Pallas kernels, down(): pl.pallas_call(functools.partial(down_kernel, jobs=count), grid=(count *...  39.5 us
    pallas_call x1, Pallas kernels, late_sum(): pl.pallas_call(functools.partial(late_kernel, experts=experts), grid=(sou...  37.2 us
    ppermute x13, starting transfers between devices, local_block(): lax.ppermute(w, 'c', swap)  33.7 us
    pallas_call x1, Pallas kernels, early_sum(): pl.pallas_call(functools.partial(early_kernel, experts=experts), grid=(so...  28.9 us
  transfers between devices with their start and end apart: 29, of which 8 were waited for; matrix products, arithmetic and copies ran while one was open for 1% of the time, Pallas kernels for 25%

profile of v1, /device:TPU:63, one launch (start us, length us, event | category | flops | bytes accessed | tf_op | source)
XLA Modules:
  0.0 772.1 jit_solution(103706641700848640)
XLA Ops:
  11.4 6.7 split_columns.1
  23.4 64.7 %collective-permute-done.5.refs_4_.refs_6_.refs_3_ = bf16[2,1,3584]{2,1,0:T(2,128)(2,1)S(1)} collective-permute-done((bf16[2,1,3584]{2,1,0:T(2,128)(2,1)S(1)}, bf16[2,1,3584]{2,1,0:T(2,128)(2,1)S(1)}, u32[]{:S(2)}, u32[]{:S(2)}) %collective-permute-start.5) | collective-permute-done | bytes 14368 | tf_op jit(solution)/shard_map/ppermute | solution.py:287
  96.5 61.9 %collective-permute-done.9.refs_2_ = bf16[768,2048]{1,0:T(8,128)(2,1)} collective-permute-done((bf16[768,2048]{1,0:T(8,128)(2,1)}, bf16[768,2048]{1,0:T(8,128)(2,1)}, u32[]{:S(2)}, u32[]{:S(2)}) %collective-permute-start.9) | collective-permute-done | bytes 3145760 | tf_op jit(solution)/shard_map/ppermute | solution.py:287
  158.8 5.1 collective-permute-start.18
  164.0 61.8 %collective-permute-done.21.refs_0_ = bf16[2048,768]{1,0:T(8,128)(2,1)} collective-permute-done((bf16[2048,768]{1,0:T(8,128)(2,1)}, bf16[2048,768]{1,0:T(8,128)(2,1)}, u32[]{:S(2)}, u32[]{:S(2)}) %collective-permute-start.21) | collective-permute-done | bytes 3145760 | tf_op jit(solution)/shard_map/ppermute | solution.py:287
  225.8 4.1 collective-permute-start.19
  233.4 59.8 %collective-permute-done.1.refs_0_ = bf16[2048,768]{1,0:T(8,128)(2,1)} collective-permute-done((bf16[2048,768]{1,0:T(8,128)(2,1)}, bf16[2048,768]{1,0:T(8,128)(2,1)}, u32[]{:S(2)}, u32[]{:S(2)}) %collective-permute-start.1) | collective-permute-done | bytes 3145760 | tf_op jit(solution)/shard_map/ppermute | solution.py:290
  295.5 17.6 %all-gather = f32[256,256]{1,0:T(8,128)S(1)} all-gather(f32[16,256]{1,0:T(8,128)S(1)} %pad_maximum_fusion.1), channel_id=2, replica_groups=mesh['z'=4,'y'=4,'x'=4,'c'=2] {'z','y'}, dimensions={0}, use_global_device_ids=true | all-gather | bytes 278528 | tf_op jit(solution)/shard_map/all_gather | solution.py:301
  318.2 2.7 slice.19
  320.9 5.1 collective-permute-start.15
  326.5 12.6 %collective-permute-start.8 = (bf16[2048,768]{1,0:T(8,128)(2,1)}, bf16[2048,768]{1,0:T(8,128)(2,1)}, u32[]{:S(2)}, u32[]{:S(2)}) collective-permute-start(bf16[2048,768]{1,0:T(8,128)(2,1)} %collective-permute-done.3.refs_1_), channel_id=1, source_target_pairs={{0,1},{1,0},{2,3},{3,2},{4,5},{5,4},{6,7},{7,6},{8,9},{9,8},{10,11... | collective-permute-start | bytes 9437192 | tf_op jit(solution)/shard_map/ppermute | solution.py:315
  339.1 20.6 %pick_rows.1 = bf16[8,16,64,2048]{3,2,1,0:T(8,128)(2,1)} custom-call(s32[16,8,256]{2,1,0:T(8,128)} %fusion.4.slot_ref, bf16[16,256,2048]{2,1,0:T(8,128)(2,1)} %bitcast.35), custom_call_target="tpu_custom_call" | custom-call | flops 8589934592 | bytes 50331648 | tf_op jit(solution)/shard_map/pick_rows/pallas_call | solution.py:86
  359.7 24.4 %gate_up.8 = (bf16[1024,384]{1,0:T(8,128)(2,1)}, bf16[1024,384]{1,0:T(8,128)(2,1)}, bf16[1024,384]{1,0:T(8,128)(2,1)}, bf16[1024,384]{1,0:T(8,128)(2,1)}) custom-call(bf16[8,1024,2048]{2,1,0:T(8,128)(2,1)} %bitcast.30, bf16[2048,768]{1,0:T(8,128)(2,1)} %collective-permute-done.refs_0_, bf16[2048,768]{1,0:T(8,128)(2,1)} %collective-permute-done.2.refs_1_, ...), custom_call_target="tpu_custom_call" | custom-call | flops 12884901888 | bytes 29360128 | tf_op jit(solution)/shard_map/gate_up/pallas_call | solution.py:124
  384.4 24.5 %gate_up.9 = (bf16[1024,384]{1,0:T(8,128)(2,1)}, bf16[1024,384]{1,0:T(8,128)(2,1)}, bf16[1024,384]{1,0:T(8,128)(2,1)}, bf16[1024,384]{1,0:T(8,128)(2,1)}) custom-call(bf16[8,1024,2048]{2,1,0:T(8,128)(2,1)} %bitcast.31, bf16[2048,768]{1,0:T(8,128)(2,1)} %collective-permute-done.21.refs_0_, bf16[2048,768]{1,0:T(8,128)(2,1)} %collective-permute-done.22.refs_1_, ...), custom_call_target="tpu_custom_call" | custom-call | flops 12884901888 | bytes 29360128 | tf_op jit(solution)/shard_map/gate_up/pallas_call | solution.py:124
  411.4 12.3 %gate_up.5 = (bf16[1024,384]{1,0:T(8,128)(2,1)}, bf16[1024,384]{1,0:T(8,128)(2,1)}) custom-call(bf16[8,1024,2048]{2,1,0:T(8,128)(2,1)} %bitcast.32, bf16[2048,768]{1,0:T(8,128)(2,1)} %collective-permute-done.1.refs_0_, bf16[2048,768]{1,0:T(8,128)(2,1)} %collective-permute-done.3.refs_1_, bf16[2,1,3584]{2,1,0:T(2,128)(2,1)} %copy-done.7, ...), custom_call_target="tpu_custom_call" | custom-call | flops 6442450944 | bytes 14680064 | tf_op jit(solution)/shard_map/gate_up/pallas_call | solution.py:124
  423.7 12.2 %gate_up.6 = (bf16[1024,384]{1,0:T(8,128)(2,1)}, bf16[1024,384]{1,0:T(8,128)(2,1)}) custom-call(bf16[8,1024,2048]{2,1,0:T(8,128)(2,1)} %bitcast.33, bf16[2048,768]{1,0:T(8,128)(2,1)} %copy-done.4, bf16[2048,768]{1,0:T(8,128)(2,1)} %collective-permute-done.8.refs_1_, bf16[2,1,3584]{2,1,0:T(2,128)(2,1)} %copy-done.7, bf16[2,1,3584]{2,1,0:T(2,128)(2,1)} %copy-done.7), custom_call_target="tpu_custom_call" | custom-call | flops 6442450944 | bytes 14680064 | tf_op jit(solution)/shard_map/gate_up/pallas_call | solution.py:124
  435.9 13.2 %down.4 = (bf16[1024,2048]{1,0:T(8,128)(2,1)}, bf16[1024,2048]{1,0:T(8,128)(2,1)}) custom-call(bf16[1024,384]{1,0:T(8,128)(2,1)} %get-tuple-element.41.refs_0_, bf16[1024,384]{1,0:T(8,128)(2,1)} %get-tuple-element.42.refs_1_, bf16[768,2048]{1,0:T(8,128)(2,1)} %collective-permute-done.9.refs_2_, bf16[2,1,3584]{2,1,0:T(2,128)(2,1)} %copy-done.12, ...), custom_call_target="tpu_custom_call" | custom-call | flops 6442450944 | bytes 14680064 | tf_op jit(solution)/shard_map/down/pallas_call | solution.py:164
  450.4 23.4 %gate_up.7 = (bf16[1024,384]{1,0:T(8,128)(2,1)}, bf16[1024,384]{1,0:T(8,128)(2,1)}, bf16[1024,384]{1,0:T(8,128)(2,1)}, bf16[1024,384]{1,0:T(8,128)(2,1)}) custom-call(bf16[8,1024,2048]{2,1,0:T(8,128)(2,1)} %bitcast.34, bf16[2048,768]{1,0:T(8,128)(2,1)} %get-tuple-element.29.refs_0_, bf16[2048,768]{1,0:T(8,128)(2,1)} %get-tuple-element.30.refs_1_, ...), custom_call_target="tpu_custom_call" | custom-call | flops 12884901888 | bytes 29360128 | tf_op jit(solution)/shard_map/gate_up/pallas_call | solution.py:124
  473.8 13.2 %down.3 = (bf16[1024,2048]{1,0:T(8,128)(2,1)}, bf16[1024,2048]{1,0:T(8,128)(2,1)}) custom-call(bf16[1024,384]{1,0:T(8,128)(2,1)} %get-tuple-element.35.refs_0_, bf16[1024,384]{1,0:T(8,128)(2,1)} %get-tuple-element.36.refs_1_, bf16[768,2048]{1,0:T(8,128)(2,1)} %bitcast.42, bf16[2,1,3584]{2,1,0:T(2,128)(2,1)} %copy-done.9, ...), custom_call_target="tpu_custom_call" | custom-call | flops 6442450944 | bytes 14680064 | tf_op jit(solution)/shard_map/down/pallas_call | solution.py:164
  487.0 13.2 %down.5 = (bf16[1024,2048]{1,0:T(8,128)(2,1)}, bf16[1024,2048]{1,0:T(8,128)(2,1)}) custom-call(bf16[1024,384]{1,0:T(8,128)(2,1)} %get-tuple-element.46.refs_0_, bf16[1024,384]{1,0:T(8,128)(2,1)} %get-tuple-element.47.refs_1_, bf16[768,2048]{1,0:T(8,128)(2,1)} %collective-permute-done.25.refs_2_, bf16[2,1,3584]{2,1,0:T(2,128)(2,1)} %copy-done.12, ...), custom_call_target="tpu_custom_call" | custom-call | flops 6442450944 | bytes 14680064 | tf_op jit(solution)/shard_map/down/pallas_call | solution.py:164
  500.2 28.9 %early_sum.1.old_ref = f32[4096,2048]{1,0:T(8,128)} custom-call(s32[16,8,256]{2,1,0:T(8,128)} %fusion.4.slot_ref, f32[16,8,256]{2,1,0:T(8,128)} %fusion.5.gate_ref, bf16[16,64,2048]{2,1,0:T(8,128)(2,1)} %bitcast.45, bf16[16,64,2048]{2,1,0:T(8,128)(2,1)} %bitcast.46, bf16[16,64,2048]{2,1,0:T(8,128)(2,1)} %bitcast.43, bf16[16,64,2048]{2,1,0:T(8,128)(2,1)} %bitcast.47, ...), custom_call_target="tpu_custom_call" | custom-call | flops 19327352832 | bytes 58720256 | tf_op jit(solution)/shard_map/early_sum/pallas_call | solution.py:202
  530.8 37.2 %late_sum.1 = f32[4096,2048]{1,0:T(8,128)} custom-call(s32[16,8,256]{2,1,0:T(8,128)} %fusion.4.slot_ref, f32[16,8,256]{2,1,0:T(8,128)} %fusion.5.gate_ref, bf16[1024,384]{1,0:T(8,128)(2,1)} %get-tuple-element.31.za0, bf16[1024,384]{1,0:T(8,128)(2,1)} %get-tuple-element.32.za1, bf16[1024,384]{1,0:T(8,128)(2,1)} %get-tuple-element.33.zb0, ...), custom_call_target="tpu_custom_call" | custom-call | flops 12884901888 | bytes 67108864 | tf_op jit(solution)/shard_map/late_sum/pallas_call | solution.py:254
  568.1 194.0 %reduce-scatter.2.cloned.1.call-done = f32[256,2048]{1,0:T(8,128)} async-done(((f32[4096,2048]{1,0:T(8,128)}), f32[256,2048]{1,0:T(8,128)}) %reduce-scatter.2.cloned.1.call-update) | async-done | bytes 2097168 | tf_op jit(solution)/shard_map/reduce_scatter | solution.py:327
  762.1 2.8 fusion.3
  (105 shorter events, 36.0 us)
Async XLA Ops:
  6.5 332.6 %all-gather.4.cloned.1.call-start = ((), (), s32[]{:S(2)}) async-start(), calls=%async_computation.2 | async-start | bytes 17825792 | tf_op jit(solution)/shard_map/all_gather | solution.py:299
  11.4 750.7 %reduce-scatter.2.cloned.1.call-start = ((), (), s32[]{:S(2)}) async-start(), calls=%async_computation.1 | async-start | bytes 35651584 | tf_op jit(solution)/shard_map/reduce_scatter | solution.py:327
  18.2 75.7 %collective-permute-start = (bf16[2048,768]{1,0:T(8,128)(2,1)}, bf16[2048,768]{1,0:T(8,128)(2,1)}, u32[]{:S(2)}, u32[]{:S(2)}) collective-permute-start(bf16[2048,768]{1,0:T(8,128)(2,1)} %get-tuple-element.29.refs_0_), channel_id=1, source_target_pairs={{0,2},{2,4},{4,6},{6,0},{1,3},{3,5},{5,7},{7,1},{8,10},{10,12},{12... | collective-permute-start | bytes 9437192 | tf_op jit(solution)/shard_map/ppermute | solution.py:287
  18.4 75.5 %collective-permute-start.2 = (bf16[2048,768]{1,0:T(8,128)(2,1)}, bf16[2048,768]{1,0:T(8,128)(2,1)}, u32[]{:S(2)}, u32[]{:S(2)}) collective-permute-start(bf16[2048,768]{1,0:T(8,128)(2,1)} %get-tuple-element.30.refs_1_), channel_id=1, source_target_pairs={{0,6},{2,0},{4,2},{6,4},{1,7},{3,1},{5,3},{7,5},{8,14},{10,8},{12,... | collective-permute-start | bytes 9437192 | tf_op jit(solution)/shard_map/ppermute | solution.py:288
  21.9 66.2 %collective-permute-start.5 = (bf16[2,1,3584]{2,1,0:T(2,128)(2,1)S(1)}, bf16[2,1,3584]{2,1,0:T(2,128)(2,1)S(1)}, u32[]{:S(2)}, u32[]{:S(2)}) collective-permute-start(bf16[2,1,3584]{2,1,0:T(2,128)(2,1)S(1)} %pad_maximum_fusion.refs_4_.refs_5_.refs_6_.refs_7_.refs_3_), channel_id=1, source_target_pairs={{0,2},{2,4},{4,6},{6,0},{1,3},{3,5},{5,7},{7,1},{8,10},{10,12},{12... | collective-permute-start | bytes 43016 | tf_op jit(solution)/shard_map/ppermute | solution.py:287
  89.5 68.9 %collective-permute-start.9 = (bf16[768,2048]{1,0:T(8,128)(2,1)}, bf16[768,2048]{1,0:T(8,128)(2,1)}, u32[]{:S(2)}, u32[]{:S(2)}) collective-permute-start(bf16[768,2048]{1,0:T(8,128)(2,1)} %bitcast.39), channel_id=1, source_target_pairs={{0,2},{2,4},{4,6},{6,0},{1,3},{3,5},{5,7},{7,1},{8,10},{10,12},{12... | collective-permute-start | bytes 9437192 | tf_op jit(solution)/shard_map/ppermute | solution.py:287
  89.5 69.3 %collective-permute-start.11 = (bf16[768,2048]{1,0:T(8,128)(2,1)}, bf16[768,2048]{1,0:T(8,128)(2,1)}, u32[]{:S(2)}, u32[]{:S(2)}) collective-permute-start(bf16[768,2048]{1,0:T(8,128)(2,1)} %bitcast.40), channel_id=1, source_target_pairs={{0,6},{2,0},{4,2},{6,4},{1,7},{3,1},{5,3},{7,5},{8,14},{10,8},{12,... | collective-permute-start | bytes 9437192 | tf_op jit(solution)/shard_map/ppermute | solution.py:288
  91.2 134.6 %collective-permute-start.21 = (bf16[2048,768]{1,0:T(8,128)(2,1)}, bf16[2048,768]{1,0:T(8,128)(2,1)}, u32[]{:S(2)}, u32[]{:S(2)}) collective-permute-start(bf16[2048,768]{1,0:T(8,128)(2,1)} %get-tuple-element.30.refs_1_), channel_id=1, source_target_pairs={{0,2},{2,4},{4,6},{6,0},{1,3},{3,5},{5,7},{7,1},{8,10},{10,12},{12... | collective-permute-start | bytes 9437192 | tf_op jit(solution)/shard_map/ppermute | solution.py:287
  93.8 136.1 %collective-permute-start.22 = (bf16[2048,768]{1,0:T(8,128)(2,1)}, bf16[2048,768]{1,0:T(8,128)(2,1)}, u32[]{:S(2)}, u32[]{:S(2)}) collective-permute-start(bf16[2048,768]{1,0:T(8,128)(2,1)} %get-tuple-element.29.refs_0_), channel_id=1, source_target_pairs={{0,6},{2,0},{4,2},{6,4},{1,7},{3,1},{5,3},{7,5},{8,14},{10,8},{12,... | collective-permute-start | bytes 9437192 | tf_op jit(solution)/shard_map/ppermute | solution.py:288
  93.8 199.4 %collective-permute-start.1 = (bf16[2048,768]{1,0:T(8,128)(2,1)}, bf16[2048,768]{1,0:T(8,128)(2,1)}, u32[]{:S(2)}, u32[]{:S(2)}) collective-permute-start(bf16[2048,768]{1,0:T(8,128)(2,1)} %collective-permute-done.refs_0_), channel_id=1, source_target_pairs={{0,2},{2,4},{4,6},{6,0},{1,3},{3,5},{5,7},{7,1},{8,10},{10,12},{12... | collective-permute-start | bytes 9437192 | tf_op jit(solution)/shard_map/ppermute | solution.py:290
  158.4 162.6 %collective-permute-start.3 = (bf16[2048,768]{1,0:T(8,128)(2,1)}, bf16[2048,768]{1,0:T(8,128)(2,1)}, u32[]{:S(2)}, u32[]{:S(2)}) collective-permute-start(bf16[2048,768]{1,0:T(8,128)(2,1)} %collective-permute-done.2.refs_1_), channel_id=1, source_target_pairs={{0,6},{2,0},{4,2},{6,4},{1,7},{3,1},{5,3},{7,5},{8,14},{10,8},{12,... | collective-permute-start | bytes 9437192 | tf_op jit(solution)/shard_map/ppermute | solution.py:291
  158.8 167.2 %collective-permute-start.18 = (bf16[2048,768]{1,0:T(8,128)(2,1)}, bf16[2048,768]{1,0:T(8,128)(2,1)}, u32[]{:S(2)}, u32[]{:S(2)}) collective-permute-start(bf16[2048,768]{1,0:T(8,128)(2,1)} %collective-permute-done.refs_0_), channel_id=1, source_target_pairs={{0,1},{1,0},{2,3},{3,2},{4,5},{5,4},{6,7},{7,6},{8,9},{9,8},{10,11... | collective-permute-start | bytes 9437192 | tf_op jit(solution)/shard_map/ppermute | solution.py:315
  225.8 100.3 %collective-permute-start.19 = (bf16[2048,768]{1,0:T(8,128)(2,1)}, bf16[2048,768]{1,0:T(8,128)(2,1)}, u32[]{:S(2)}, u32[]{:S(2)}) collective-permute-start(bf16[2048,768]{1,0:T(8,128)(2,1)} %collective-permute-done.2.refs_1_), channel_id=1, source_target_pairs={{0,1},{1,0},{2,3},{3,2},{4,5},{5,4},{6,7},{7,6},{8,9},{9,8},{10,11... | collective-permute-start | bytes 9437192 | tf_op jit(solution)/shard_map/ppermute | solution.py:315
  229.9 96.6 %collective-permute-start.23 = (bf16[2048,768]{1,0:T(8,128)(2,1)}, bf16[2048,768]{1,0:T(8,128)(2,1)}, u32[]{:S(2)}, u32[]{:S(2)}) collective-permute-start(bf16[2048,768]{1,0:T(8,128)(2,1)} %collective-permute-done.21.refs_0_), channel_id=1, source_target_pairs={{0,1},{1,0},{2,3},{3,2},{4,5},{5,4},{6,7},{7,6},{8,9},{9,8},{10,11... | collective-permute-start | bytes 9437192 | tf_op jit(solution)/shard_map/ppermute | solution.py:315
  293.2 90.9 %collective-permute-start.24 = (bf16[2048,768]{1,0:T(8,128)(2,1)}, bf16[2048,768]{1,0:T(8,128)(2,1)}, u32[]{:S(2)}, u32[]{:S(2)}) collective-permute-start(bf16[2048,768]{1,0:T(8,128)(2,1)} %collective-permute-done.22.refs_1_), channel_id=1, source_target_pairs={{0,1},{1,0},{2,3},{3,2},{4,5},{5,4},{6,7},{7,6},{8,9},{9,8},{10,11... | collective-permute-start | bytes 9437192 | tf_op jit(solution)/shard_map/ppermute | solution.py:315
  320.9 87.9 %collective-permute-start.15 = (bf16[2048,768]{1,0:T(8,128)(2,1)}, bf16[2048,768]{1,0:T(8,128)(2,1)}, u32[]{:S(2)}, u32[]{:S(2)}) collective-permute-start(bf16[2048,768]{1,0:T(8,128)(2,1)} %get-tuple-element.29.refs_0_), channel_id=1, source_target_pairs={{0,1},{1,0},{2,3},{3,2},{4,5},{5,4},{6,7},{7,6},{8,9},{9,8},{10,11... | collective-permute-start | bytes 9437192 | tf_op jit(solution)/shard_map/ppermute | solution.py:315
  326.0 84.2 %collective-permute-start.16 = (bf16[2048,768]{1,0:T(8,128)(2,1)}, bf16[2048,768]{1,0:T(8,128)(2,1)}, u32[]{:S(2)}, u32[]{:S(2)}) collective-permute-start(bf16[2048,768]{1,0:T(8,128)(2,1)} %get-tuple-element.30.refs_1_), channel_id=1, source_target_pairs={{0,1},{1,0},{2,3},{3,2},{4,5},{5,4},{6,7},{7,6},{8,9},{9,8},{10,11... | collective-permute-start | bytes 9437192 | tf_op jit(solution)/shard_map/ppermute | solution.py:315
  326.1 84.3 %collective-permute-start.7 = (bf16[2048,768]{1,0:T(8,128)(2,1)}, bf16[2048,768]{1,0:T(8,128)(2,1)S(1)}, u32[]{:S(2)}, u32[]{:S(2)}) collective-permute-start(bf16[2048,768]{1,0:T(8,128)(2,1)} %collective-permute-done.1.refs_0_), channel_id=1, source_target_pairs={{0,1},{1,0},{2,3},{3,2},{4,5},{5,4},{6,7},{7,6},{8,9},{9,8},{10,11... | collective-permute-start | bytes 9437192 | tf_op jit(solution)/shard_map/ppermute | solution.py:315
  326.5 84.7 %collective-permute-start.8 = (bf16[2048,768]{1,0:T(8,128)(2,1)}, bf16[2048,768]{1,0:T(8,128)(2,1)}, u32[]{:S(2)}, u32[]{:S(2)}) collective-permute-start(bf16[2048,768]{1,0:T(8,128)(2,1)} %collective-permute-done.3.refs_1_), channel_id=1, source_target_pairs={{0,1},{1,0},{2,3},{3,2},{4,5},{5,4},{6,7},{7,6},{8,9},{9,8},{10,11... | collective-permute-start | bytes 9437192 | tf_op jit(solution)/shard_map/ppermute | solution.py:315
  384.1 89.7 %collective-permute-start.17 = (bf16[768,2048]{1,0:T(8,128)(2,1)}, bf16[768,2048]{1,0:T(8,128)(2,1)}, u32[]{:S(2)}, u32[]{:S(2)}) collective-permute-start(bf16[768,2048]{1,0:T(8,128)(2,1)} %bitcast.41), channel_id=1, source_target_pairs={{0,1},{1,0},{2,3},{3,2},{4,5},{5,4},{6,7},{7,6},{8,9},{9,8},{10,11... | collective-permute-start | bytes 9437192 | tf_op jit(solution)/shard_map/ppermute | solution.py:315
  410.4 76.6 %collective-permute-start.25 = (bf16[768,2048]{1,0:T(8,128)(2,1)}, bf16[768,2048]{1,0:T(8,128)(2,1)}, u32[]{:S(2)}, u32[]{:S(2)}) collective-permute-start(bf16[768,2048]{1,0:T(8,128)(2,1)} %collective-permute-done.9.refs_2_), channel_id=1, source_target_pairs={{0,1},{1,0},{2,3},{3,2},{4,5},{5,4},{6,7},{7,6},{8,9},{9,8},{10,11... | collective-permute-start | bytes 9437192 | tf_op jit(solution)/shard_map/ppermute | solution.py:315
  411.3 75.7 %collective-permute-start.26 = (bf16[768,2048]{1,0:T(8,128)(2,1)}, bf16[768,2048]{1,0:T(8,128)(2,1)}, u32[]{:S(2)}, u32[]{:S(2)}) collective-permute-start(bf16[768,2048]{1,0:T(8,128)(2,1)} %collective-permute-done.11.refs_6_), channel_id=1, source_target_pairs={{0,1},{1,0},{2,3},{3,2},{4,5},{5,4},{6,7},{7,6},{8,9},{9,8},{10,11... | collective-permute-start | bytes 9437192 | tf_op jit(solution)/shard_map/ppermute | solution.py:315
  449.1 80.1 %collective-permute-start.13 = (bf16[384,2048]{1,0:T(8,128)(2,1)}, bf16[384,2048]{1,0:T(8,128)(2,1)S(1)}, u32[]{:S(2)}, u32[]{:S(2)}) collective-permute-start(bf16[384,2048]{1,0:T(8,128)(2,1)} %collective-permute-done.10.wa0), channel_id=1, source_target_pairs={{0,1},{1,0},{2,3},{3,2},{4,5},{5,4},{6,7},{7,6},{8,9},{9,8},{10,11... | collective-permute-start | bytes 4718600 | tf_op jit(solution)/shard_map/ppermute | solution.py:315
  450.1 79.1 %collective-permute-start.14 = (bf16[384,2048]{1,0:T(8,128)(2,1)}, bf16[384,2048]{1,0:T(8,128)(2,1)S(1)}, u32[]{:S(2)}, u32[]{:S(2)}) collective-permute-start(bf16[384,2048]{1,0:T(8,128)(2,1)} %collective-permute-done.12.wa1), channel_id=1, source_target_pairs={{0,1},{1,0},{2,3},{3,2},{4,5},{5,4},{6,7},{7,6},{8,9},{9,8},{10,11... | collective-permute-start | bytes 4718600 | tf_op jit(solution)/shard_map/ppermute | solution.py:315
  (20 other events, 2442.4 us)
Sparse Core Ops, SparseCore 0:
  11.5 111.4 all-gather.3
  568.2 193.8 reduce-scatter.1
